TPU v7x, 256 devices: a whole 4x4x8 slice. The times are simulated.
256 devices in a mesh: row: 16 (over x, y), col: 16 (over z, core).
Axes of the slice: x: 4, y: 4, z: 8, core: 2. Of those that a mesh axis runs over, the one named last changes fastest.
Arguments:
- inputs: bfloat16 [2048, 16384], P('col', 'row'), may hold values from -6 to 6
- weight: bfloat16 [16384, 16384], P('row', 'col'), may hold values from -0.046875 to 0.046875
- cotangent: bfloat16 [2048, 16384], P('row', 'col'), may hold values from -0.75 to 0.75
- scale_in: float32 [8, 16384], P(None, 'row'), may hold values from -4 to 4
- scale_out: float32 [8, 16384], P(None, 'col'), may hold values from -4 to 4
- member: int32 [2048], replicated, may hold values from 0 to 7
Outputs:
- input_grad: bfloat16 [2048, 16384], P('col', 'row')
- weight_grad: float32 [16384, 16384], P('row', 'col')
- in_factor_grad: float32 [8, 16384], P(None, 'row')
- out_factor_grad: float32 [8, 16384], P(None, 'col')
All inputs are finite; a program needn't handle non-finite values.
Results may differ from a plain program's by a relative error of at most 0.0049.
Values may be sent and summed in bfloat16 or wider, within the bound.
No kernel may reach another device: no remote copies, remote signals or barrier semaphores. Data moves between devices by JAX's collectives and lax.ppermute only.
A program may use at most 128 MiB of HBM per device.

v0:
```python
import jax
import jax.numpy as jnp
from jax import lax
from jax.sharding import PartitionSpec as P

highest = lax.Precision.HIGHEST


def from_everyone(value, axis):
    copies = jnp.broadcast_to(value, (lax.axis_size(axis), *value.shape))
    return lax.all_to_all(copies, axis, split_axis=0, concat_axis=0, tiled=True)


def of_everyone(value, axis):
    return from_everyone(value, axis).sum(axis=0)


def gathered_total(value, axis):
    return lax.all_gather(value, axis).sum(0)


def member_sums(one_hot, values):
    return jnp.dot(one_hot.T, values, precision=highest)


def local(inputs, weight, cotangent, scale_in, scale_out, member):
    n_members = scale_in.shape[0]
    one_hot = (member[:, None] == jnp.arange(n_members, dtype=jnp.int32)[None, :]).astype(
        jnp.float32
    )
    full_inputs = lax.all_gather(inputs, "col", axis=0, tiled=True)
    full_cot = lax.all_gather(cotangent, "row", axis=0, tiled=True)
    r_rows = jnp.dot(one_hot, scale_in, precision=highest)
    s_rows = jnp.dot(one_hot, scale_out, precision=highest)
    scaled_in = (full_inputs * r_rows).astype(jnp.bfloat16)
    scaled_cot = (full_cot * s_rows).astype(jnp.bfloat16)
    batch = scaled_in.shape[0]
    pre_part = jnp.dot(scaled_in, weight, preferred_element_type=jnp.float32)
    out_term = member_sums(one_hot, full_cot.astype(jnp.float32) * pre_part)
    out_factor_grad = of_everyone(out_term, "row")
    col_share = batch // lax.axis_size("col")
    col_start = lax.axis_index("col") * col_share
    back_part = lax.dot_general(
        scaled_cot, weight, (((1,), (1,)), ((), ())), preferred_element_type=jnp.float32
    )
    in_term = member_sums(one_hot, full_inputs.astype(jnp.float32) * back_part)
    in_factor_grad = gathered_total(in_term, "col")
    back_block = lax.psum_scatter(back_part, "col", scatter_dimension=0, tiled=True)
    r_block = lax.dynamic_slice_in_dim(r_rows, col_start, col_share, 0)
    input_grad = (back_block * r_block).astype(jnp.bfloat16)
    weight_grad = lax.dot_general(
        scaled_in, scaled_cot, (((0,), (0,)), ((), ())), preferred_element_type=jnp.float32
    )
    return (input_grad, weight_grad, in_factor_grad, out_factor_grad)


def solution(mesh):
    placed = (
        P("col", "row"),
        P("row", "col"),
        P("row", "col"),
        P(None, "row"),
        P(None, "col"),
        P(),
    )
    return jax.shard_map(
        local,
        mesh=mesh,
        in_specs=placed,
        out_specs=(P("col", "row"), P("row", "col"), P(None, "row"), P(None, "col")),
        check_vma=False,
    )
```

profile of v0, /device:TPU:2, one launch (start us, length us, event | category | flops | bytes accessed | tf_op | source)
XLA Modules:
  0.0 195.8 jit_solution(3907940686163401925)
XLA Ops:
  7.2 0.0 copy-start
  7.2 0.0 all-gather.4.cloned.1.call-start
  7.2 0.7 all-gather.4.cloned.1.call-update
  7.9 0.0 all-gather.6.cloned.1.call-start
  8.0 0.7 all-gather.6.cloned.1.call-update
  8.7 0.0 reduce-scatter.2.cloned.1.call-start
  8.7 61.1 %all-gather.4.cloned.1.call-done = bf16[2048,1024]{1,0:T(8,128)(2,1)} async-done(((bf16[128,1024]{1,0:T(8,128)(2,1)}), bf16[2048,1024]{1,0:T(8,128)(2,1)}) %all-gather.4.cloned.1.call-update) | async-done | bytes 4194320 | tf_op jit(solution)/shard_map/all_gather | solution.py:32
  69.8 5.6 %fusion = bf16[2048,1024]{1,0:T(8,128)(2,1)S(1)} fusion(bf16[2048,1024]{1,0:T(8,128)(2,1)} %all-gather.4.cloned.1.call-done, f32[8,1024]{1,0:T(8,128)} %param.10, s32[2048]{0:T(1024)} %param.11), kind=kOutput, calls=%fused_computation.4 | convolution fusion | flops 207634432 | bytes 8429568 | tf_op jit(solution)/shard_map/dot_general | solution.py:34
  75.4 0.0 copy-start.2
  75.4 2.0 copy-done.2
  77.4 0.0 copy-done
  77.4 7.1 %fusion.13 = f32[2048,1024]{1,0:T(8,128)} fusion(bf16[2048,1024]{1,0:T(8,128)(2,1)S(1)} %fusion, bf16[1024,1024]{1,0:T(8,128)(2,1)S(1)} %copy-done), kind=kOutput, calls=%fused_computation.18 | convolution fusion | flops 4294967296 | bytes 14680064 | tf_op jit(solution)/shard_map/dot_general | solution.py:43
  84.4 0.0 copy-start.4
  84.4 0.0 reduce-scatter.2.cloned.1.call-update
  84.5 0.7 copy-done.4
  85.1 0.1 copy-done.5
  85.2 5.6 %fusion.4 = f32[2048,1024]{1,0:T(8,128)} fusion(f32[8,1024]{1,0:T(8,128)S(1)} %copy-done.5, s32[2048]{0:T(1024)S(1)} %copy-done.4), kind=kOutput, calls=%fused_computation.9 | convolution fusion | flops 201342976 | bytes 8429568 | tf_op jit(solution)/shard_map/dot_general | solution.py:33
  90.8 22.5 %all-gather.6.cloned.1.call-done = bf16[2048,1024]{1,0:T(8,128)(2,1)} async-done(((bf16[128,1024]{1,0:T(8,128)(2,1)}), bf16[2048,1024]{1,0:T(8,128)(2,1)}) %all-gather.6.cloned.1.call-update) | async-done | bytes 4194320 | tf_op jit(solution)/shard_map/all_gather | solution.py:31
  113.3 7.7 %fusion.9 = f32[2048,1024]{1,0:T(8,128)S(1)} fusion(bf16[1024,1024]{1,0:T(8,128)(2,1)S(1)} %copy-done, f32[2048,1024]{1,0:T(8,128)} %fusion.4, bf16[2048,1024]{1,0:T(8,128)(2,1)} %all-gather.6.cloned.1.call-done), kind=kOutput, calls=%fused_computation.16 | convolution fusion | flops 4301258752 | bytes 23068672 | tf_op jit(solution)/shard_map/dot_general | solution.py:38
  121.0 0.0 copy-done.1
  121.0 3.4 %fusion.1 = f32[8,1024]{1,0:T(8,128)S(1)} fusion(f32[2048,1024]{1,0:T(8,128)S(1)} %fusion.9, bf16[2048,1024]{1,0:T(8,128)(2,1)S(1)} %copy-done.1, s32[2048]{0:T(1024)S(1)} %copy-done.4), kind=kOutput, calls=%fused_computation.5 | convolution fusion | flops 205537280 | bytes 12623872 | tf_op jit(solution)/shard_map/dot_general | solution.py:23
  124.5 0.9 broadcast_in_dim.2
  125.3 7.3 %all-to-all-start = ((f32[16,8,1024]{2,1,0:T(8,128)}), f32[16,8,1024]{2,1,0:T(8,128)S(1)}, u32[]{:S(2)}, u32[]{:S(2)}) async-start(f32[16,8,1024]{2,1,0:T(8,128)} %broadcast_in_dim.2), calls=%async_computation.1 | async-start | bytes 1048576 | tf_op jit(solution)/shard_map/all_to_all | solution.py:11
  132.6 12.9 %fusion.11 = f32[1024,1024]{1,0:T(8,128)} fusion(bf16[2048,1024]{1,0:T(8,128)(2,1)} %copy-done.2, f32[2048,1024]{1,0:T(8,128)} %fusion.4, bf16[2048,1024]{1,0:T(8,128)(2,1)} %all-gather.6.cloned.1.call-done), kind=kOutput, calls=%fused_computation.17 | convolution fusion | flops 4301258752 | bytes 20971520 | tf_op jit(solution)/shard_map/dot_general | solution.py:51
  145.5 0.0 copy-done.3
  145.5 5.9 %fusion.3 = f32[8,1024]{1,0:T(8,128)S(1)} fusion(f32[2048,1024]{1,0:T(8,128)} %fusion.13, bf16[2048,1024]{1,0:T(8,128)(2,1)S(1)} %copy-done.3, s32[2048]{0:T(1024)S(1)} %copy-done.4), kind=kOutput, calls=%fused_computation.7 | convolution fusion | flops 205537280 | bytes 12623872 | tf_op jit(solution)/shard_map/dot_general | solution.py:23
  151.4 18.8 %all-gather = f32[128,1024]{1,0:T(8,128)S(1)} all-gather(f32[8,1024]{1,0:T(8,128)S(1)} %fusion.3), channel_id=2, replica_groups=mesh['row'=16,'col'=16] {'col'}, dimensions={0}, use_global_device_ids=true | all-gather | bytes 557056 | tf_op jit(solution)/shard_map/all_gather | solution.py:19
  170.2 0.6 bitcast_reduce_fusion
  170.9 0.0 all-to-all-done
  170.9 0.6 reduce_sum.19
  171.5 15.8 %reduce-scatter.2.cloned.1.call-done = f32[128,1024]{1,0:T(8,128)} async-done(((f32[2048,1024]{1,0:T(8,128)}), f32[128,1024]{1,0:T(8,128)}) %reduce-scatter.2.cloned.1.call-update) | async-done | bytes 524304 | tf_op jit(solution)/shard_map/reduce_scatter | solution.py:48
  187.4 2.0 %multiply_convert_fusion = bf16[128,1024]{1,0:T(8,128)(2,1)} fusion(f32[128,1024]{1,0:T(8,128)} %reduce-scatter.2.cloned.1.call-done, f32[2048,1024]{1,0:T(8,128)} %fusion.4, s32[]{:T(128)S(6)} %select_n.3), kind=kLoop, calls=%fused_computation.11 | loop fusion | flops 262144 | bytes 1310724 | tf_op jit(solution)/shard_map/convert_element_type | solution.py:50
  (3 shorter events, 0.0 us)
Async XLA Ops:
  7.2 70.2 %copy-start = (bf16[1024,1024]{1,0:T(8,128)(2,1)S(1)}, bf16[1024,1024]{1,0:T(8,128)(2,1)}, u32[]{:S(2)}) copy-start(bf16[1024,1024]{1,0:T(8,128)(2,1)} %param.7) | copy-start | bytes 6291460
  7.2 62.6 %all-gather.4.cloned.1.call-start = ((), (), s32[]{:S(2)}) async-start(), calls=%async_computation.2 | async-start | bytes 4456448 | tf_op jit(solution)/shard_map/all_gather | solution.py:32
  7.9 105.4 %all-gather.6.cloned.1.call-start = ((), (), s32[]{:S(2)}) async-start(), calls=%async_computation.4 | async-start | bytes 4456448 | tf_op jit(solution)/shard_map/all_gather | solution.py:31
  8.7 178.7 %reduce-scatter.2.cloned.1.call-start = ((), (), s32[]{:S(2)}) async-start(), calls=%async_computation.3 | async-start | bytes 8912896 | tf_op jit(solution)/shard_map/reduce_scatter | solution.py:48
  75.4 2.0 %copy-start.2 = (bf16[2048,1024]{1,0:T(8,128)(2,1)}, bf16[2048,1024]{1,0:T(8,128)(2,1)S(1)}, u32[]{:S(2)}) copy-start(bf16[2048,1024]{1,0:T(8,128)(2,1)S(1)} %fusion) | copy-start | bytes 12582916
  84.4 0.7 copy-start.4
  84.4 0.8 copy-start.5
  113.3 7.7 %copy-start.1 = (bf16[2048,1024]{1,0:T(8,128)(2,1)S(1)}, bf16[2048,1024]{1,0:T(8,128)(2,1)}, u32[]{:S(2)}) copy-start(bf16[2048,1024]{1,0:T(8,128)(2,1)} %all-gather.4.cloned.1.call-done) | copy-start | bytes 12582916
  125.3 45.5 %all-to-all-start = ((f32[16,8,1024]{2,1,0:T(8,128)}), f32[16,8,1024]{2,1,0:T(8,128)S(1)}, u32[]{:S(2)}, u32[]{:S(2)}) async-start(f32[16,8,1024]{2,1,0:T(8,128)} %broadcast_in_dim.2), calls=%async_computation.1 | async-start | bytes 1048576 | tf_op jit(solution)/shard_map/all_to_all | solution.py:11
  132.6 12.9 %copy-start.3 = (bf16[2048,1024]{1,0:T(8,128)(2,1)S(1)}, bf16[2048,1024]{1,0:T(8,128)(2,1)}, u32[]{:S(2)}) copy-start(bf16[2048,1024]{1,0:T(8,128)(2,1)} %all-gather.6.cloned.1.call-done) | copy-start | bytes 12582916
Sparse Core Ops, SparseCore 0:
  10.4 59.3 all-gather.3
  71.7 41.6 all-gather.5
  115.9 71.4 reduce-scatter.1
where the time goes:
time: 196 us
  waiting for transfers between devices  101 us (52%)
  matrix products  48.2 us (25%)
  blocking collectives  18.8 us (10%)
  between operations  13.8 us (7%)
  starting transfers between devices  7.39 us (4%)
  local copies, waits for them, and re-layouts  3.59 us (2%)
  other arithmetic  3.25 us (2%)
    all_gather x1, waiting for transfers between devices, local(): full_cot = lax.all_gather(cotangent, 'row', axis=0, tiled=True)  61.1 us
    all_gather x1, waiting for transfers between devices, local(): full_inputs = lax.all_gather(inputs, 'col', axis=0, tiled=True)  22.5 us
    all_gather x1, blocking collectives, gathered_total(): return lax.all_gather(value, axis).sum(0)  18.8 us
    reduce_scatter x1, waiting for transfers between devices, local(): lax.psum_scatter(back_part, 'col', scatter_dimension=0, tiled=True)  15.8 us
    dot_general x1, matrix products, local(): lax.dot_general(scaled_in, scaled_cot, (((0,), (0,)), ((), ())), preferre...  12.9 us
    dot_general x2, matrix products, member_sums(): return jnp.dot(one_hot.T, values, precision=highest)  9.29 us
    dot_general x1, matrix products, local(): pre_part = jnp.dot(scaled_in, weight, preferred_element_type=jnp.float32)  7.7 us
    all_to_all x1, starting transfers between devices, from_everyone(): return lax.all_to_all(copies, axis, split_axis=0, concat_axis=0, tiled=True)  7.28 us
  transfers between devices with their start and end apart: 4, of which 3 were waited for; matrix products, arithmetic and copies ran while one was open for 26% of the time, Pallas kernels for 0%

commit v1 on v0

--- a/solution.py
+++ b/solution.py
@@ -4,6 +4,12 @@
 from jax.sharding import PartitionSpec as P
 
 highest = lax.Precision.HIGHEST
+
+
+def _set_sheet(local_array, bus_axis):
+    a_next = jnp.stack([local_array] * lax.psum(1, bus_axis), axis=0)
+    response = lax.all_to_all(a_next, axis_name=bus_axis, split_axis=0, concat_axis=0)
+    return jnp.concatenate(response, axis=0)
 
 
 def from_everyone(value, axis):
@@ -28,7 +34,7 @@
     one_hot = (member[:, None] == jnp.arange(n_members, dtype=jnp.int32)[None, :]).astype(
         jnp.float32
     )
-    full_inputs = lax.all_gather(inputs, "col", axis=0, tiled=True)
+    full_inputs = _set_sheet(inputs, "col")
     full_cot = lax.all_gather(cotangent, "row", axis=0, tiled=True)
     r_rows = jnp.dot(one_hot, scale_in, precision=highest)
     s_rows = jnp.dot(one_hot, scale_out, precision=highest)

time: 196 us -> 279 us (1.42)
  waiting for transfers between devices: 101 us -> 177 us
  starting transfers between devices: 7.39 us -> 12.4 us
  matrix products: 48.2 us -> 44.8 us
    all_to_all x0 -> x1, waiting for transfers between devices: none -> 114 us  [_set_sheet(): lax.all_to_all(a_next, axis_name=bus_axis, split_axis=0, concat_axis=0)]
    all_gather x1 -> x0, waiting for transfers between devices: 22.5 us -> none  [local(): full_inputs = lax.all_gather(inputs, 'col', axis=0, tiled=True)]
    reduce_scatter x1, waiting for transfers between devices: 15.8 us -> 0.01 us  [local(): lax.psum_scatter(back_part, 'col', scatter_dimension=0, tiled=True)]
    all_to_all x0 -> x1, starting transfers between devices: none -> 7.32 us  [_set_sheet(): lax.all_to_all(a_next, axis_name=bus_axis, split_axis=0, concat_axis=0)]
    dot_general x1, matrix products: 7.7 us -> 4.53 us  [local(): pre_part = jnp.dot(scaled_in, weight, preferred_element_type=jnp.float32)]
  transfers between devices with their start and end apart: 4 -> 4, of which waited for: 3 -> 2; matrix products, arithmetic and copies ran while one was open for 26% -> 13% of each run, Pallas kernels for 0% -> 0%
where the time goes in v1:
time: 279 us; the launch traced here: 277 us
  waiting for transfers between devices  177 us (63%)
  matrix products  44.8 us (16%)
  blocking collectives  19.4 us (7%)
  between operations  14.1 us (5%)
  starting transfers between devices  12.4 us (4%)
  local copies, waits for them, and re-layouts  6.32 us (2%)
  other arithmetic  3.25 us (1%)
    all_to_all x1, waiting for transfers between devices, _set_sheet(): lax.all_to_all(a_next, axis_name=bus_axis, split_axis=0, concat_axis=0)  114 us
    all_gather x1, waiting for transfers between devices, local(): full_cot = lax.all_gather(cotangent, 'row', axis=0, tiled=True)  61.9 us
    all_gather x1, blocking collectives, gathered_total(): return lax.all_gather(value, axis).sum(0)  19.4 us
    dot_general x1, matrix products, local(): lax.dot_general(scaled_in, scaled_cot, (((0,), (0,)), ((), ())), preferre...  10.2 us
    dot_general x2, matrix products, member_sums(): return jnp.dot(one_hot.T, values, precision=highest)  9.83 us
    dot_general x1, matrix products, local(): r_rows = jnp.dot(one_hot, scale_in, precision=highest)  7.54 us
    all_to_all x1, starting transfers between devices, _set_sheet(): lax.all_to_all(a_next, axis_name=bus_axis, split_axis=0, concat_axis=0)  7.32 us
    dot_general x1, matrix products, local(): lax.dot_general(scaled_cot, weight, (((1,), (1,)), ((), ())), preferred_e...  7.12 us
  transfers between devices with their start and end apart: 4, of which 2 were waited for; matrix products, arithmetic and copies ran while one was open for 13% of the time, Pallas kernels for 0%

profile of v1, /device:TPU:2, one launch (start us, length us, event | category | flops | bytes accessed | tf_op | source)
XLA Modules:
  0.0 277.3 jit_solution(3898294739384454740)
XLA Ops:
  7.2 0.0 copy-start
  7.2 0.0 all-gather.3.cloned.1.call-start
  7.2 0.7 all-gather.3.cloned.1.call-update
  7.9 0.0 reduce-scatter.2.cloned.1.call-start
  8.0 61.9 %all-gather.3.cloned.1.call-done = bf16[2048,1024]{1,0:T(8,128)(2,1)} async-done(((bf16[128,1024]{1,0:T(8,128)(2,1)}), bf16[2048,1024]{1,0:T(8,128)(2,1)}) %all-gather.3.cloned.1.call-update) | async-done | bytes 4194320 | tf_op jit(solution)/shard_map/all_gather | solution.py:38
  69.8 5.6 %fusion = bf16[2048,1024]{1,0:T(8,128)(2,1)S(1)} fusion(bf16[2048,1024]{1,0:T(8,128)(2,1)} %all-gather.3.cloned.1.call-done, f32[8,1024]{1,0:T(8,128)} %param.10, s32[2048]{0:T(1024)} %param.11), kind=kOutput, calls=%fused_computation.4 | convolution fusion | flops 207634432 | bytes 8429568 | tf_op jit(solution)/shard_map/dot_general | solution.py:40
  75.4 0.0 copy-start.2
  75.4 1.9 copy-done.2
  77.4 0.0 copy-done
  77.4 7.1 %fusion.9 = f32[2048,1024]{1,0:T(8,128)} fusion(bf16[2048,1024]{1,0:T(8,128)(2,1)S(1)} %fusion, bf16[1024,1024]{1,0:T(8,128)(2,1)S(1)} %copy-done), kind=kOutput, calls=%fused_computation.16 | convolution fusion | flops 4294967296 | bytes 14680064 | tf_op jit(solution)/shard_map/dot_general | solution.py:49
  84.5 0.0 copy-start.5
  84.5 0.0 reduce-scatter.2.cloned.1.call-update
  84.5 0.9 copy-done.5
  85.4 2.5 stack.2
  88.0 7.3 %all-to-all-start = ((bf16[16,128,1024]{2,1,0:T(8,128)(2,1)}), bf16[16,128,1024]{2,1,0:T(8,128)(2,1)}, u32[]{:S(2)}, u32[]{:S(2)}) async-start(bf16[16,128,1024]{2,1,0:T(8,128)(2,1)} %stack.2), calls=%async_computation.1 | async-start | bytes 8388608 | tf_op jit(solution)/shard_map/all_to_all | solution.py:11
  95.3 114.5 %all-to-all-done = bf16[16,128,1024]{2,1,0:T(8,128)(2,1)} async-done(((bf16[16,128,1024]{2,1,0:T(8,128)(2,1)}), bf16[16,128,1024]{2,1,0:T(8,128)(2,1)}, u32[]{:S(2)}, u32[]{:S(2)}) %all-to-all-start) | async-done | bytes 4194336 | tf_op jit(solution)/shard_map/all_to_all | solution.py:11
  209.8 0.0 copy-done.4
  209.8 0.0 copy-done.6
  209.8 7.5 %fusion.2 = (bf16[2048,1024]{1,0:T(8,128)(2,1)S(1)}, f32[2048,1024]{1,0:T(8,128)}) fusion(bf16[16,128,1024]{2,1,0:T(8,128)(2,1)} %all-to-all-done, f32[8,1024]{1,0:T(8,128)S(1)} %copy-done.6, s32[2048]{0:T(1024)S(1)} %copy-done.4), kind=kOutput, calls=%fused_computation.6 | convolution fusion | flops 207634432 | bytes 16818176 | tf_op jit(solution)/shard_map/dot_general | solution.py:39
  217.3 4.5 %fusion.11 = f32[2048,1024]{1,0:T(8,128)S(1)} fusion(bf16[2048,1024]{1,0:T(8,128)(2,1)S(1)} %get-tuple-element.4, bf16[1024,1024]{1,0:T(8,128)(2,1)S(1)} %copy-done), kind=kOutput, calls=%fused_computation.18 | convolution fusion | flops 4294967296 | bytes 14680064 | tf_op jit(solution)/shard_map/dot_general | solution.py:44
  221.9 0.0 copy-done.3
  221.9 0.0 copy-done.1
  221.9 3.4 %fusion.1 = f32[8,1024]{1,0:T(8,128)S(1)} fusion(f32[2048,1024]{1,0:T(8,128)S(1)} %fusion.11, bf16[2048,1024]{1,0:T(8,128)(2,1)S(1)} %copy-done.1, s32[2048]{0:T(1024)S(1)} %copy-done.4), kind=kOutput, calls=%fused_computation.5 | convolution fusion | flops 205537280 | bytes 12623872 | tf_op jit(solution)/shard_map/dot_general | solution.py:29
  225.3 0.9 broadcast_in_dim.2
  226.2 5.0 %all-to-all-start.1 = ((f32[16,8,1024]{2,1,0:T(8,128)}), f32[16,8,1024]{2,1,0:T(8,128)S(1)}, u32[]{:S(2)}, u32[]{:S(2)}) async-start(f32[16,8,1024]{2,1,0:T(8,128)} %broadcast_in_dim.2), calls=%async_computation.2 | async-start | bytes 1048576 | tf_op jit(solution)/shard_map/all_to_all | solution.py:17
  231.2 10.2 %fusion.10 = f32[1024,1024]{1,0:T(8,128)} fusion(bf16[2048,1024]{1,0:T(8,128)(2,1)} %copy-done.3, bf16[2048,1024]{1,0:T(8,128)(2,1)} %copy-done.2), kind=kOutput, calls=%fused_computation.17 | convolution fusion | flops 4294967296 | bytes 12582912 | tf_op jit(solution)/shard_map/dot_general | solution.py:57
  241.4 6.4 %fusion.3 = f32[8,1024]{1,0:T(8,128)S(1)} fusion(f32[2048,1024]{1,0:T(8,128)} %fusion.9, bf16[2048,1024]{1,0:T(8,128)(2,1)} %bitcast.1, s32[2048]{0:T(1024)S(1)} %copy-done.4), kind=kOutput, calls=%fused_computation.7 | convolution fusion | flops 205537280 | bytes 12623872 | tf_op jit(solution)/shard_map/dot_general | solution.py:29
  247.8 19.4 %all-gather = f32[128,1024]{1,0:T(8,128)S(1)} all-gather(f32[8,1024]{1,0:T(8,128)S(1)} %fusion.3), channel_id=2, replica_groups=mesh['row'=16,'col'=16] {'col'}, dimensions={0}, use_global_device_ids=true | all-gather | bytes 557056 | tf_op jit(solution)/shard_map/all_gather | solution.py:25
  267.2 0.6 bitcast_reduce_fusion
  267.8 0.0 all-to-all-done.1
  267.8 0.6 reduce_sum.19
  268.5 2.0 multiply_convert_fusion
  (5 shorter events, 0.0 us)
Async XLA Ops:
  7.2 70.2 %copy-start = (bf16[1024,1024]{1,0:T(8,128)(2,1)S(1)}, bf16[1024,1024]{1,0:T(8,128)(2,1)}, u32[]{:S(2)}) copy-start(bf16[1024,1024]{1,0:T(8,128)(2,1)} %param.7) | copy-start | bytes 6291460
  7.2 62.6 %all-gather.3.cloned.1.call-start = ((), (), s32[]{:S(2)}) async-start(), calls=%async_computation.3 | async-start | bytes 4456448 | tf_op jit(solution)/shard_map/all_gather | solution.py:38
  7.9 260.6 %reduce-scatter.2.cloned.1.call-start = ((), (), s32[]{:S(2)}) async-start(), calls=%async_computation.4 | async-start | bytes 8912896 | tf_op jit(solution)/shard_map/reduce_scatter | solution.py:54
  75.4 1.9 copy-start.2
  84.5 0.9 copy-start.5
  88.0 121.8 %copy-start.4 = (s32[2048]{0:T(1024)S(1)}, s32[2048]{0:T(1024)}, u32[]{:S(2)}) copy-start(s32[2048]{0:T(1024)} %param.11) | copy-start | bytes 24580
  88.0 121.8 %copy-start.6 = (f32[8,1024]{1,0:T(8,128)S(1)}, f32[8,1024]{1,0:T(8,128)}, u32[]{:S(2)}) copy-start(f32[8,1024]{1,0:T(8,128)} %param.9) | copy-start | bytes 98308
  88.0 121.8 %all-to-all-start = ((bf16[16,128,1024]{2,1,0:T(8,128)(2,1)}), bf16[16,128,1024]{2,1,0:T(8,128)(2,1)}, u32[]{:S(2)}, u32[]{:S(2)}) async-start(bf16[16,128,1024]{2,1,0:T(8,128)(2,1)} %stack.2), calls=%async_computation.1 | async-start | bytes 8388608 | tf_op jit(solution)/shard_map/all_to_all | solution.py:11
  217.3 4.5 %copy-start.3 = (bf16[2048,1024]{1,0:T(8,128)(2,1)}, bf16[2048,1024]{1,0:T(8,128)(2,1)S(1)}, u32[]{:S(2)}) copy-start(bf16[2048,1024]{1,0:T(8,128)(2,1)S(1)} %get-tuple-element.4) | copy-start | bytes 12582916
  217.3 4.5 %copy-start.1 = (bf16[2048,1024]{1,0:T(8,128)(2,1)S(1)}, bf16[2048,1024]{1,0:T(8,128)(2,1)}, u32[]{:S(2)}) copy-start(bf16[2048,1024]{1,0:T(8,128)(2,1)} %all-gather.3.cloned.1.call-done) | copy-start | bytes 12582916
  226.2 41.6 %all-to-all-start.1 = ((f32[16,8,1024]{2,1,0:T(8,128)}), f32[16,8,1024]{2,1,0:T(8,128)S(1)}, u32[]{:S(2)}, u32[]{:S(2)}) async-start(f32[16,8,1024]{2,1,0:T(8,128)} %broadcast_in_dim.2), calls=%async_computation.2 | async-start | bytes 1048576 | tf_op jit(solution)/shard_map/all_to_all | solution.py:17
Sparse Core Ops, SparseCore 0:
  10.4 59.3 all-gather.2
  84.6 155.0 reduce-scatter.1
